TPU v7x, 256 devices: a whole 4x4x8 slice. The times are simulated.
256 devices in a mesh: data: 32 (over z, y_hi, core), width: 8 (over y_lo, x).
Axes of the slice: x: 4, y: 4 (y_hi: 2, y_lo: 2; y = y_hi * 2 + y_lo), z: 8, core: 2. Of those that a mesh axis runs over, the one named last changes fastest.
Arguments:
- slope_up: float32 [32, 1280, 5120], P('data', None, 'width'), may hold values from -1.25 to 1.25
- slope_down: float32 [32, 5120, 1280], P('data', 'width'), may hold values from -1.25 to 1.25
- slope_query: float32 [32, 1280, 1280], P('data', None, 'width'), may hold values from -1.25 to 1.25
- slope_key: float32 [32, 1280, 1280], P('data', None, 'width'), may hold values from -1.25 to 1.25
- slope_value: float32 [32, 1280, 1280], P('data', None, 'width'), may hold values from -1.25 to 1.25
- slope_mixed: float32 [32, 1280, 1280], P('data', 'width'), may hold values from -1.25 to 1.25
- slope_norm: float32 [32, 1280], P('data'), may hold values from -12 to 12
- slope_bias: float32 [32, 1280], P('data'), may hold values from -12 to 12
- param_up: float32 [1280, 5120], P('data', 'width'), may hold values from -0.15625 to 0.15625
- param_down: float32 [5120, 1280], P('width', 'data'), may hold values from -0.078125 to 0.078125
- param_query: float32 [1280, 1280], P('data', 'width'), may hold values from -0.15625 to 0.15625
- param_key: float32 [1280, 1280], P('data', 'width'), may hold values from -0.15625 to 0.15625
- param_value: float32 [1280, 1280], P('data', 'width'), may hold values from -0.15625 to 0.15625
- param_mixed: float32 [1280, 1280], P('width', 'data'), may hold values from -0.15625 to 0.15625
- param_norm: float32 [1280], P('data'), may hold values from 0.25 to 1.75
- param_bias: float32 [1280], P('data'), may hold values from -3 to 3
- state_up: float32 [1280, 5120], P('data', 'width'), may hold values from -1.75 to 1.75
- state_down: float32 [5120, 1280], P('width', 'data'), may hold values from -1.75 to 1.75
- state_query: float32 [1280, 1280], P('data', 'width'), may hold values from -1.75 to 1.75
- state_key: float32 [1280, 1280], P('data', 'width'), may hold values from -1.75 to 1.75
- state_value: float32 [1280, 1280], P('data', 'width'), may hold values from -1.75 to 1.75
- state_mixed: float32 [1280, 1280], P('width', 'data'), may hold values from -1.75 to 1.75
- state_norm: float32 [1280], P('data'), may hold values from -1.75 to 1.75
- state_bias: float32 [1280], P('data'), may hold values from -1.75 to 1.75
Outputs:
- half_up: bfloat16 [1280, 5120], P(None, 'width')
- half_down: bfloat16 [5120, 1280], P('width')
- half_query: bfloat16 [1280, 1280], P(None, 'width')
- half_key: bfloat16 [1280, 1280], P(None, 'width')
- half_value: bfloat16 [1280, 1280], P(None, 'width')
- half_mixed: bfloat16 [1280, 1280], P('width')
- half_norm: bfloat16 [1280], replicated
- half_bias: bfloat16 [1280], replicated
- next_up: float32 [1280, 5120], P('data', 'width')
- next_down: float32 [5120, 1280], P('width', 'data')
- next_query: float32 [1280, 1280], P('data', 'width')
- next_key: float32 [1280, 1280], P('data', 'width')
- next_value: float32 [1280, 1280], P('data', 'width')
- next_mixed: float32 [1280, 1280], P('width', 'data')
- next_norm: float32 [1280], P('data')
- next_bias: float32 [1280], P('data')
- state_new_up: float32 [1280, 5120], P('data', 'width')
- state_new_down: float32 [5120, 1280], P('width', 'data')
- state_new_query: float32 [1280, 1280], P('data', 'width')
- state_new_key: float32 [1280, 1280], P('data', 'width')
- state_new_value: float32 [1280, 1280], P('data', 'width')
- state_new_mixed: float32 [1280, 1280], P('width', 'data')
- state_new_norm: float32 [1280], P('data')
- state_new_bias: float32 [1280], P('data')
All inputs are finite; a program needn't handle non-finite values.
Results may differ from a plain program's by a relative error of at most 0.0085.
Values may be sent and summed in bfloat16 or wider, within the bound.
No kernel may reach another device: no remote copies, remote signals or barrier semaphores. Data moves between devices by JAX's collectives and lax.ppermute only.
A program may use at most 128 MiB of HBM per device.

v0:
```python
import jax
import jax.numpy as jnp
from jax import lax
from jax.sharding import PartitionSpec as P

learn_rate = 0.1
hold_rate = 0.8


def in_blocks(shard, dim, peers):
    shape = shard.shape
    parts = shard.reshape(*shape[:dim], peers, shape[dim] // peers, *shape[dim + 1 :])
    return jnp.moveaxis(parts, dim, 0)


def sum_together(arrays, axis, dims):
    peers = lax.axis_size(axis)
    parts = [in_blocks(a, dim, peers) for a, dim in zip(arrays, dims)]
    lines = jnp.concatenate([b.reshape(peers, -1) for b in parts], axis=1)
    extent = max(16, -(-lines.shape[1] // 1024) * 8)
    lines = jnp.pad(lines, ((0, 0), (0, extent * 128 - lines.shape[1]))).reshape(-1, 128)
    vector, at, gathered = (lax.psum_scatter(lines, axis, tiled=True).reshape(-1), 0, [])
    for b in parts:
        part = b[0]
        gathered.append(vector[at : at + part.size].reshape(part.shape))
        at += part.size
    return tuple(gathered)


def turned_gather(arrays, axis, dims):
    turned = [jnp.moveaxis(a, dim, 0) for a, dim in zip(arrays, dims)]
    widths = [t[0].size for t in turned]
    both = jnp.concatenate([t.reshape(-1, w) for t, w in zip(turned, widths)], axis=1)
    whole = lax.all_gather(both, axis, axis=0, tiled=True)
    parts = jnp.split(whole, [sum(widths[:k]) for k in range(1, len(widths))], axis=1)
    return tuple(
        (
            jnp.moveaxis(b.reshape(-1, *t.shape[1:]), 0, dim)
            for b, t, dim in zip(parts, turned, dims)
        )
    )


def on_device(
    slope_up,
    slope_down,
    slope_query,
    slope_key,
    slope_value,
    slope_mixed,
    slope_norm,
    slope_bias,
    param_up,
    param_down,
    param_query,
    param_key,
    param_value,
    param_mixed,
    param_norm,
    param_bias,
    state_up,
    state_down,
    state_query,
    state_key,
    state_value,
    state_mixed,
    state_norm,
    state_bias,
):
    mean_up, mean_down, mean_query, mean_key, mean_value, mean_mixed, mean_norm, mean_bias = (
        sum_together(
            (
                slope_up[0],
                slope_down[0],
                slope_query[0],
                slope_key[0],
                slope_value[0],
                slope_mixed[0],
                slope_norm[0],
                slope_bias[0],
            ),
            "data",
            (0, 1, 0, 0, 0, 1, 0, 0),
        )
    )
    mean_rate = lax.axis_size("data") ** (-0.5)
    mean_up = mean_up * mean_rate
    mean_down = mean_down * mean_rate
    mean_query = mean_query * mean_rate
    mean_key = mean_key * mean_rate
    mean_value = mean_value * mean_rate
    mean_mixed = mean_mixed * mean_rate
    mean_norm = mean_norm * mean_rate
    mean_bias = mean_bias * mean_rate
    state_new_up = hold_rate * state_up + mean_up
    next_up = param_up - learn_rate * state_new_up
    state_new_down = hold_rate * state_down + mean_down
    next_down = param_down - learn_rate * state_new_down
    state_new_query = hold_rate * state_query + mean_query
    next_query = param_query - learn_rate * state_new_query
    state_new_key = hold_rate * state_key + mean_key
    next_key = param_key - learn_rate * state_new_key
    state_new_value = hold_rate * state_value + mean_value
    next_value = param_value - learn_rate * state_new_value
    state_new_mixed = hold_rate * state_mixed + mean_mixed
    next_mixed = param_mixed - learn_rate * state_new_mixed
    state_new_norm = hold_rate * state_norm + mean_norm
    next_norm = param_norm - learn_rate * state_new_norm
    state_new_bias = hold_rate * state_bias + mean_bias
    next_bias = param_bias - learn_rate * state_new_bias
    half_up, half_down, half_query, half_key, half_value, half_mixed, half_norm, half_bias = (
        turned_gather(
            (
                next_up.astype(jnp.bfloat16),
                next_down.astype(jnp.bfloat16),
                next_query.astype(jnp.bfloat16),
                next_key.astype(jnp.bfloat16),
                next_value.astype(jnp.bfloat16),
                next_mixed.astype(jnp.bfloat16),
                next_norm.astype(jnp.bfloat16),
                next_bias.astype(jnp.bfloat16),
            ),
            "data",
            (0, 1, 0, 0, 0, 1, 0, 0),
        )
    )
    return (
        half_up,
        half_down,
        half_query,
        half_key,
        half_value,
        half_mixed,
        half_norm,
        half_bias,
        next_up,
        next_down,
        next_query,
        next_key,
        next_value,
        next_mixed,
        next_norm,
        next_bias,
        state_new_up,
        state_new_down,
        state_new_query,
        state_new_key,
        state_new_value,
        state_new_mixed,
        state_new_norm,
        state_new_bias,
    )


def solution(mesh):
    return jax.shard_map(
        on_device,
        mesh=mesh,
        in_specs=(
            P("data", None, "width"),
            P("data", "width", None),
            P("data", None, "width"),
            P("data", None, "width"),
            P("data", None, "width"),
            P("data", "width", None),
            P("data", None),
            P("data", None),
            P("data", "width"),
            P("width", "data"),
            P("data", "width"),
            P("data", "width"),
            P("data", "width"),
            P("width", "data"),
            P("data"),
            P("data"),
            P("data", "width"),
            P("width", "data"),
            P("data", "width"),
            P("data", "width"),
            P("data", "width"),
            P("width", "data"),
            P("data"),
            P("data"),
        ),
        out_specs=(
            P(None, "width"),
            P("width", None),
            P(None, "width"),
            P(None, "width"),
            P(None, "width"),
            P("width", None),
            P(),
            P(),
            P("data", "width"),
            P("width", "data"),
            P("data", "width"),
            P("data", "width"),
            P("data", "width"),
            P("width", "data"),
            P("data"),
            P("data"),
            P("data", "width"),
            P("width", "data"),
            P("data", "width"),
            P("data", "width"),
            P("data", "width"),
            P("width", "data"),
            P("data"),
            P("data"),
        ),
        check_vma=False,
    )
```

profile of v0, /device:TPU:1, one launch (start us, length us, event | category | flops | bytes accessed | tf_op | source)
XLA Modules:
  0.0 367.7 jit_solution(9540244367930635654)
XLA Ops:
  7.2 0.0 reduce-scatter.2.cloned.1.call-start
  7.2 3.5 copy.87
  10.7 6.0 %copy.88 = f32[32,640,40]{2,1,0:T(8,128)} copy(f32[32,640,40]{1,2,0:T(8,128)S(1)} %bitcast.19) | data formatting | bytes 6553600 | tf_op jit(solution)/shard_map/transpose | solution.py:13
  16.7 10.0 %reshape.102 = f32[32,25600]{1,0:T(8,128)} reshape(f32[32,640,40]{2,1,0:T(8,128)} %copy.88) | data formatting | bytes 6553600 | tf_op jit(solution)/shard_map/reshape | solution.py:19
  26.7 2.2 reshape_reshape_squeeze.12
  28.9 1.9 constant_dynamic-update-slice_fusion.5
  30.8 2.6 copy.89
  33.4 2.9 reshape_reshape_squeeze.13
  36.4 2.6 copy.90
  39.0 2.8 reshape_reshape_squeeze.14
  41.7 2.6 copy.91
  44.3 2.8 reshape_reshape_squeeze.15
  47.1 2.6 copy.92
  49.7 3.0 copy.93
  52.7 3.8 %reshape.103 = f32[32,6400]{1,0:T(8,128)} reshape(f32[32,160,40]{2,1,0:T(8,128)} %copy.93) | data formatting | bytes 1638400 | tf_op jit(solution)/shard_map/reshape | solution.py:19
  56.5 0.1 reshape_squeeze.14
  56.6 0.1 reshape_squeeze.15
  56.8 0.0 copy-start.2
  56.8 1.9 constant_dynamic-update-slice_fusion.4
  58.7 2.1 constant_dynamic-update-slice_fusion.3
  60.8 2.1 constant_dynamic-update-slice_fusion.2
  62.9 1.0 constant_dynamic-update-slice_fusion.1
  63.9 0.9 constant_dynamic-update-slice_fusion
  64.8 1.3 dynamic-update-slice.6
  66.1 1.4 dynamic-update-slice.7
  67.5 8.3 %pad.4 = f32[32,77824]{1,0:T(8,128)} pad(f32[32,76880]{1,0:T(8,128)} %dynamic-update-slice.7, f32[]{:T(128)} %constant.5.clone.1), padding=0_0x0_944 | pad | bytes 19802116 | tf_op jit(solution)/shard_map/jit(_pad)/pad | solution.py:21
  75.8 8.2 %reshape.104 = f32[19456,128]{1,0:T(8,128)} reshape(f32[32,77824]{1,0:T(8,128)} %pad.4) | data formatting | bytes 19922944 | tf_op jit(solution)/shard_map/reshape | solution.py:21
  84.0 0.0 copy-start.7
  84.0 0.0 copy-start.8
  84.1 0.0 copy-start.3
  84.1 0.0 copy-start.4
  84.1 0.0 copy-start.11
  84.1 0.0 copy-start.12
  84.2 0.0 reduce-scatter.2.cloned.1.call-update
  84.2 0.2 all-gather.2.cloned.1.call-start
  84.4 160.1 %reduce-scatter.2.cloned.1.call-done = f32[608,128]{1,0:T(8,128)} async-done(((f32[19456,128]{1,0:T(8,128)}), f32[608,128]{1,0:T(8,128)}) %reduce-scatter.2.cloned.1.call-update) | async-done | bytes 311312 | tf_op jit(solution)/shard_map/reduce_scatter | solution.py:22
  244.6 0.8 slice_multiply_fusion.2
  245.4 0.1 mul.132
  245.5 0.1 mul.136
  245.6 0.1 mul.141
  245.7 0.1 copy.95
  245.8 0.1 mul.128
  245.9 1.4 convert_bitcast_fusion.2
  247.3 0.1 copy.96
  247.4 0.1 copy.97
  247.5 1.0 slice_multiply_fusion
  248.4 0.2 mul.123
  248.7 0.1 copy.94
  248.9 0.6 convert_bitcast_fusion.1
  249.5 0.6 fusion.6
  250.2 0.7 convert_bitcast_fusion
  250.9 0.7 fusion.7
  251.6 0.7 fusion.4
  252.3 0.8 concatenate.7
  253.1 0.0 all-gather.2.cloned.1.call-update
  253.1 93.3 %all-gather.2.cloned.1.call-done = bf16[1280,1922]{1,0:T(8,128)(2,1)} async-done(((bf16[40,1922]{1,0:T(8,128)(2,1)}), bf16[1280,1922]{1,0:T(8,128)(2,1)}) %all-gather.2.cloned.1.call-update) | async-done | bytes 4920336 | tf_op jit(solution)/shard_map/all_gather | solution.py:34
  346.4 3.1 slice_bitcast_fusion.1
  349.4 1.0 copy.100
  350.4 1.0 copy.101
  351.4 1.0 copy.102
  352.3 1.0 copy.99
  353.3 3.4 slice_bitcast_fusion
  356.7 2.2 copy.98
  358.8 2.0 slice_reduce_fusion
  (38 shorter events, 0.2 us)
Async XLA Ops:
  7.2 237.4 %reduce-scatter.2.cloned.1.call-start = ((), (), s32[]{:S(2)}) async-start(), calls=%async_computation.1 | async-start | bytes 10272768 | tf_op jit(solution)/shard_map/reduce_scatter | solution.py:22
  33.4 23.1 %copy-start.15 = (f32[1,1280]{1,0:T(1,128)S(1)}, f32[1,1280]{1,0:T(1,128)}, u32[]{:S(2)}) copy-start(f32[1,1280]{1,0:T(1,128)} %param.30) | copy-start | bytes 15364
  33.4 23.2 %copy-start.16 = (f32[1,1280]{1,0:T(1,128)S(1)}, f32[1,1280]{1,0:T(1,128)}, u32[]{:S(2)}) copy-start(f32[1,1280]{1,0:T(1,128)} %param.31) | copy-start | bytes 15364
  33.4 23.3 %copy-start = (f32[32,25600]{1,0:T(8,128)S(1)}, f32[32,25600]{1,0:T(8,128)}, u32[]{:S(2)}) copy-start(f32[32,25600]{1,0:T(8,128)} %reshape.102) | copy-start | bytes 9830404
  56.7 6.1 %copy-start.1 = (f32[32,6400]{1,0:T(8,128)S(1)}, f32[32,6400]{1,0:T(8,128)}, u32[]{:S(2)}) copy-start(f32[32,6400]{1,0:T(8,128)} %reshape_reshape_squeeze.15) | copy-start | bytes 2457604
  56.8 7.1 %copy-start.2 = (f32[32,6400]{1,0:T(8,128)S(1)}, f32[32,6400]{1,0:T(8,128)}, u32[]{:S(2)}) copy-start(f32[32,6400]{1,0:T(8,128)} %reshape.103) | copy-start | bytes 2457604
  84.0 161.9 %copy-start.17 = (f32[40]{0:T(128)S(1)}, f32[40]{0:T(128)}, u32[]{:S(2)}) copy-start(f32[40]{0:T(128)} %param.39) | copy-start | bytes 484
  84.0 161.9 %copy-start.18 = (f32[40]{0:T(128)S(1)}, f32[40]{0:T(128)}, u32[]{:S(2)}) copy-start(f32[40]{0:T(128)} %param.47) | copy-start | bytes 484
  84.0 161.9 %copy-start.19 = (f32[40]{0:T(128)S(1)}, f32[40]{0:T(128)}, u32[]{:S(2)}) copy-start(f32[40]{0:T(128)} %param.38) | copy-start | bytes 484
  84.0 161.9 %copy-start.20 = (f32[40]{0:T(128)S(1)}, f32[40]{0:T(128)}, u32[]{:S(2)}) copy-start(f32[40]{0:T(128)} %param.46) | copy-start | bytes 484
  84.0 164.8 %copy-start.7 = (f32[160,40]{0,1:T(8,128)S(1)}, f32[160,40]{0,1:T(8,128)}, u32[]{:S(2)}) copy-start(f32[160,40]{0,1:T(8,128)} %param.37) | copy-start | bytes 76804
  84.0 164.8 %copy-start.8 = (f32[160,40]{0,1:T(8,128)S(1)}, f32[160,40]{0,1:T(8,128)}, u32[]{:S(2)}) copy-start(f32[160,40]{0,1:T(8,128)} %param.45) | copy-start | bytes 76804
  84.1 165.5 %copy-start.9 = (f32[40,160]{1,0:T(8,128)S(1)}, f32[40,160]{1,0:T(8,128)}, u32[]{:S(2)}) copy-start(f32[40,160]{1,0:T(8,128)} %param.34) | copy-start | bytes 76804
  84.1 165.4 %copy-start.10 = (f32[40,160]{1,0:T(8,128)S(1)}, f32[40,160]{1,0:T(8,128)}, u32[]{:S(2)}) copy-start(f32[40,160]{1,0:T(8,128)} %param.42) | copy-start | bytes 76804
  84.1 166.1 %copy-start.3 = (f32[640,40]{0,1:T(8,128)S(1)}, f32[640,40]{0,1:T(8,128)}, u32[]{:S(2)}) copy-start(f32[640,40]{0,1:T(8,128)} %param.33) | copy-start | bytes 307204
  84.1 166.1 %copy-start.4 = (f32[640,40]{0,1:T(8,128)S(1)}, f32[640,40]{0,1:T(8,128)}, u32[]{:S(2)}) copy-start(f32[640,40]{0,1:T(8,128)} %param.41) | copy-start | bytes 307204
  84.1 166.8 %copy-start.5 = (f32[40,640]{1,0:T(8,128)S(1)}, f32[40,640]{1,0:T(8,128)}, u32[]{:S(2)}) copy-start(f32[40,640]{1,0:T(8,128)} %param.32) | copy-start | bytes 307204
  84.1 166.8 %copy-start.6 = (f32[40,640]{1,0:T(8,128)S(1)}, f32[40,640]{1,0:T(8,128)}, u32[]{:S(2)}) copy-start(f32[40,640]{1,0:T(8,128)} %param.40) | copy-start | bytes 307204
  84.1 167.5 %copy-start.11 = (f32[40,160]{1,0:T(8,128)S(1)}, f32[40,160]{1,0:T(8,128)}, u32[]{:S(2)}) copy-start(f32[40,160]{1,0:T(8,128)} %param.36) | copy-start | bytes 76804
  84.1 167.4 %copy-start.12 = (f32[40,160]{1,0:T(8,128)S(1)}, f32[40,160]{1,0:T(8,128)}, u32[]{:S(2)}) copy-start(f32[40,160]{1,0:T(8,128)} %param.44) | copy-start | bytes 76804
  84.2 167.4 %copy-start.13 = (f32[40,160]{1,0:T(8,128)S(1)}, f32[40,160]{1,0:T(8,128)}, u32[]{:S(2)}) copy-start(f32[40,160]{1,0:T(8,128)} %param.35) | copy-start | bytes 76804
  84.2 167.4 %copy-start.14 = (f32[40,160]{1,0:T(8,128)S(1)}, f32[40,160]{1,0:T(8,128)}, u32[]{:S(2)}) copy-start(f32[40,160]{1,0:T(8,128)} %param.43) | copy-start | bytes 76804
  84.2 262.2 %all-gather.2.cloned.1.call-start = ((), (), s32[]{:S(2)}) async-start(), calls=%async_computation.2 | async-start | bytes 5406720 | tf_op jit(solution)/shard_map/all_gather | solution.py:34
Sparse Core Ops, SparseCore 0:
  84.3 160.2 reduce-scatter.1
  253.2 93.1 all-gather.1
where the time goes:
time: 369 us; the launch traced here: 368 us
  waiting for transfers between devices  253 us (69%)
  local copies, waits for them, and re-layouts  93 us (25%)
  between operations  14.4 us (4%)
  other arithmetic  6.58 us (2%)
    reduce_scatter x1, waiting for transfers between devices, sum_together(): lax.psum_scatter(lines, axis, tiled=True).reshape(-1)  160 us
    all_gather x1, waiting for transfers between devices, turned_gather(): whole = lax.all_gather(both, axis, axis=0, tiled=True)  93.3 us
    unnamed x59, local copies, waits for them, and re-layouts  31.3 us
    reshape x2, local copies, waits for them, and re-layouts, sum_together(): lines = jnp.concatenate([b.reshape(peers, -1) for b in parts], axis=1)  13.8 us
    another operation x4, local copies, waits for them, and re-layouts, sum_together(): lines = jnp.concatenate([b.reshape(peers, -1) for b in parts], axis=1)  10.6 us
    transpose x2, local copies, waits for them, and re-layouts, in_blocks(): return jnp.moveaxis(parts, dim, 0)  9.01 us
    pad x1, local copies, waits for them, and re-layouts, sum_together(): jnp.pad(lines, ((0, 0), (0, extent * 128 - lines.shape[1])))  8.25 us
    reshape x1, local copies, waits for them, and re-layouts, sum_together(): jnp.pad(lines, ((0, 0), (0, extent * 128 - lines.shape[1])))  8.22 us
  transfers between devices with their start and end apart: 2, of which 2 were waited for; matrix products, arithmetic and copies ran while one was open for 0% of the time, Pallas kernels for 0%

commit v1 on v0

--- a/solution.py
+++ b/solution.py
@@ -5,6 +5,11 @@
 
 learn_rate = 0.1
 hold_rate = 0.8
+
+
+def all_by_exchange(value, axis, along):
+    sent = jnp.stack([value] * lax.axis_size(axis))
+    return jnp.concatenate(lax.all_to_all(sent, axis, 0, 0), axis=along)
 
 
 def in_blocks(shard, dim, peers):
@@ -31,7 +36,7 @@
     turned = [jnp.moveaxis(a, dim, 0) for a, dim in zip(arrays, dims)]
     widths = [t[0].size for t in turned]
     both = jnp.concatenate([t.reshape(-1, w) for t, w in zip(turned, widths)], axis=1)
-    whole = lax.all_gather(both, axis, axis=0, tiled=True)
+    whole = all_by_exchange(both, axis, 0)
     parts = jnp.split(whole, [sum(widths[:k]) for k in range(1, len(widths))], axis=1)
     return tuple(
         (

time: 369 us -> 403 us (1.092)
  blocking collectives: 0 us -> 129 us
  waiting for transfers between devices: 253 us -> 160 us
    all_to_all x0 -> x1, blocking collectives: none -> 129 us  [all_by_exchange(): return jnp.concatenate(lax.all_to_all(sent, axis, 0, 0), axis=along)]
    all_gather x1 -> x0, waiting for transfers between devices: 93.3 us -> none  [turned_gather(): whole = lax.all_gather(both, axis, axis=0, tiled=True)]
  transfers between devices with their start and end apart: 2 -> 1, of which waited for: 2 -> 1; matrix products, arithmetic and copies ran while one was open for 0% -> 0% of each run, Pallas kernels for 0% -> 0%
where the time goes in v1:
time: 403 us; the launch traced here: 401 us
  waiting for transfers between devices  160 us (40%)
  blocking collectives  129 us (32%)
  local copies, waits for them, and re-layouts  91.5 us (23%)
  between operations  14.4 us (4%)
  other arithmetic  6.57 us (2%)
    reduce_scatter x1, waiting for transfers between devices, sum_together(): lax.psum_scatter(lines, axis, tiled=True).reshape(-1)  160 us
    all_to_all x1, blocking collectives, all_by_exchange(): return jnp.concatenate(lax.all_to_all(sent, axis, 0, 0), axis=along)  129 us
    unnamed x59, local copies, waits for them, and re-layouts  33.6 us
    reshape x2, local copies, waits for them, and re-layouts, sum_together(): lines = jnp.concatenate([b.reshape(peers, -1) for b in parts], axis=1)  13.8 us
    another operation x4, local copies, waits for them, and re-layouts, sum_together(): lines = jnp.concatenate([b.reshape(peers, -1) for b in parts], axis=1)  10.6 us
    transpose x2, local copies, waits for them, and re-layouts, in_blocks(): return jnp.moveaxis(parts, dim, 0)  9.15 us
    pad x1, local copies, waits for them, and re-layouts, sum_together(): jnp.pad(lines, ((0, 0), (0, extent * 128 - lines.shape[1])))  8.25 us
    reshape x1, local copies, waits for them, and re-layouts, sum_together(): jnp.pad(lines, ((0, 0), (0, extent * 128 - lines.shape[1])))  8.24 us
  transfers between devices with their start and end apart: 1, of which 1 were waited for; matrix products, arithmetic and copies ran while one was open for 0% of the time, Pallas kernels for 0%

profile of v1, /device:TPU:1, one launch (start us, length us, event | category | flops | bytes accessed | tf_op | source)
XLA Modules:
  0.0 401.4 jit_solution(12864839686089982369)
XLA Ops:
  7.2 0.0 reduce-scatter.2.cloned.1.call-start
  7.2 3.5 copy.89
  10.7 6.1 %copy.90 = f32[32,640,40]{2,1,0:T(8,128)} copy(f32[32,640,40]{1,2,0:T(8,128)S(1)} %bitcast.23) | data formatting | bytes 6553600 | tf_op jit(solution)/shard_map/transpose | solution.py:18
  16.8 10.0 %reshape.107 = f32[32,25600]{1,0:T(8,128)} reshape(f32[32,640,40]{2,1,0:T(8,128)} %copy.90) | data formatting | bytes 6553600 | tf_op jit(solution)/shard_map/reshape | solution.py:24
  26.8 2.2 reshape_reshape_squeeze.12
  29.0 1.9 constant_dynamic-update-slice_fusion.5
  31.0 2.6 copy.91
  33.6 2.9 reshape_reshape_squeeze.13
  36.5 2.6 copy.92
  39.1 2.8 reshape_reshape_squeeze.14
  41.8 2.6 copy.93
  44.4 2.8 reshape_reshape_squeeze.15
  47.2 2.6 copy.94
  49.8 3.0 copy.95
  52.9 3.8 reshape.108
  56.7 0.1 reshape_squeeze.14
  56.8 0.1 reshape_squeeze.15
  56.9 0.0 copy-start.2
  56.9 1.9 constant_dynamic-update-slice_fusion.4
  58.8 2.1 constant_dynamic-update-slice_fusion.3
  61.0 2.1 constant_dynamic-update-slice_fusion.2
  63.1 1.0 constant_dynamic-update-slice_fusion.1
  64.0 1.0 constant_dynamic-update-slice_fusion
  65.0 1.3 dynamic-update-slice.6
  66.4 1.4 dynamic-update-slice.7
  67.8 8.3 %pad.4 = f32[32,77824]{1,0:T(8,128)} pad(f32[32,76880]{1,0:T(8,128)} %dynamic-update-slice.7, f32[]{:T(128)} %constant.5.clone.1), padding=0_0x0_944 | pad | bytes 19802116 | tf_op jit(solution)/shard_map/jit(_pad)/pad | solution.py:26
  76.0 8.2 %reshape.109 = f32[19456,128]{1,0:T(8,128)} reshape(f32[32,77824]{1,0:T(8,128)} %pad.4) | data formatting | bytes 19922944 | tf_op jit(solution)/shard_map/reshape | solution.py:26
  84.3 0.0 copy-start.7
  84.3 0.0 copy-start.8
  84.3 0.0 copy-start.10
  84.3 0.0 copy-start.3
  84.4 0.0 copy-start.6
  84.4 0.0 copy-start.11
  84.4 0.0 copy-start.14
  84.4 0.0 reduce-scatter.2.cloned.1.call-update
  84.4 160.4 %reduce-scatter.2.cloned.1.call-done = f32[608,128]{1,0:T(8,128)} async-done(((f32[19456,128]{1,0:T(8,128)}), f32[608,128]{1,0:T(8,128)}) %reduce-scatter.2.cloned.1.call-update) | async-done | bytes 311312 | tf_op jit(solution)/shard_map/reduce_scatter | solution.py:27
  244.8 0.8 slice_multiply_fusion.2
  245.7 0.1 mul.132
  245.8 0.1 mul.136
  245.8 0.1 mul.141
  245.9 0.1 copy.97
  246.0 0.1 mul.128
  246.1 1.3 convert_bitcast_fusion.2
  247.5 0.1 copy.98
  247.6 0.1 copy.99
  247.7 1.0 slice_multiply_fusion
  248.7 0.2 mul.123
  248.9 0.1 copy.96
  249.1 0.6 convert_bitcast_fusion.1
  249.7 0.6 fusion.6
  250.4 0.7 convert_bitcast_fusion
  251.1 0.7 fusion.7
  251.8 0.7 fusion.4
  252.5 0.1 concatenate.7
  252.6 0.6 stack.2
  253.3 128.6 %all_to_all.5 = bf16[32,40,1922]{2,1,0:T(8,128)(2,1)S(1)} all-to-all(bf16[32,40,1922]{2,1,0:T(8,128)(2,1)S(1)} %stack.2), channel_id=1, replica_groups=mesh['data'=32,'width'=8] {'data'}, dimensions={0} | all-to-all | bytes 9840640 | tf_op jit(solution)/shard_map/all_to_all | solution.py:12
  381.9 2.0 slice_bitcast_fusion.1
  383.9 1.5 slice_bitcast_fusion
  385.4 1.0 slice_reduce_fusion
  386.4 2.1 copy.101
  388.4 2.1 copy.102
  390.5 1.0 copy.103
  391.4 1.0 copy.104
  392.4 2.2 copy.100
  (37 shorter events, 0.2 us)
Async XLA Ops:
  7.2 237.6 %reduce-scatter.2.cloned.1.call-start = ((), (), s32[]{:S(2)}) async-start(), calls=%async_computation.2 | async-start | bytes 10272768 | tf_op jit(solution)/shard_map/reduce_scatter | solution.py:27
  33.6 23.1 %copy-start.15 = (f32[1,1280]{1,0:T(1,128)S(1)}, f32[1,1280]{1,0:T(1,128)}, u32[]{:S(2)}) copy-start(f32[1,1280]{1,0:T(1,128)} %param.30) | copy-start | bytes 15364
  33.6 23.2 %copy-start.16 = (f32[1,1280]{1,0:T(1,128)S(1)}, f32[1,1280]{1,0:T(1,128)}, u32[]{:S(2)}) copy-start(f32[1,1280]{1,0:T(1,128)} %param.31) | copy-start | bytes 15364
  33.6 23.3 %copy-start = (f32[32,25600]{1,0:T(8,128)S(1)}, f32[32,25600]{1,0:T(8,128)}, u32[]{:S(2)}) copy-start(f32[32,25600]{1,0:T(8,128)} %reshape.107) | copy-start | bytes 9830404
  56.9 6.2 %copy-start.1 = (f32[32,6400]{1,0:T(8,128)S(1)}, f32[32,6400]{1,0:T(8,128)}, u32[]{:S(2)}) copy-start(f32[32,6400]{1,0:T(8,128)} %reshape_reshape_squeeze.15) | copy-start | bytes 2457604
  56.9 7.1 %copy-start.2 = (f32[32,6400]{1,0:T(8,128)S(1)}, f32[32,6400]{1,0:T(8,128)}, u32[]{:S(2)}) copy-start(f32[32,6400]{1,0:T(8,128)} %reshape.108) | copy-start | bytes 2457604
  84.3 161.9 %copy-start.17 = (f32[40]{0:T(128)S(1)}, f32[40]{0:T(128)}, u32[]{:S(2)}) copy-start(f32[40]{0:T(128)} %param.39) | copy-start | bytes 484
  84.3 161.9 %copy-start.18 = (f32[40]{0:T(128)S(1)}, f32[40]{0:T(128)}, u32[]{:S(2)}) copy-start(f32[40]{0:T(128)} %param.47) | copy-start | bytes 484
  84.3 161.9 %copy-start.19 = (f32[40]{0:T(128)S(1)}, f32[40]{0:T(128)}, u32[]{:S(2)}) copy-start(f32[40]{0:T(128)} %param.38) | copy-start | bytes 484
  84.3 161.9 %copy-start.20 = (f32[40]{0:T(128)S(1)}, f32[40]{0:T(128)}, u32[]{:S(2)}) copy-start(f32[40]{0:T(128)} %param.46) | copy-start | bytes 484
  84.3 164.8 %copy-start.7 = (f32[160,40]{0,1:T(8,128)S(1)}, f32[160,40]{0,1:T(8,128)}, u32[]{:S(2)}) copy-start(f32[160,40]{0,1:T(8,128)} %param.37) | copy-start | bytes 76804
  84.3 164.8 %copy-start.8 = (f32[160,40]{0,1:T(8,128)S(1)}, f32[160,40]{0,1:T(8,128)}, u32[]{:S(2)}) copy-start(f32[160,40]{0,1:T(8,128)} %param.45) | copy-start | bytes 76804
  84.3 165.4 %copy-start.9 = (f32[40,160]{1,0:T(8,128)S(1)}, f32[40,160]{1,0:T(8,128)}, u32[]{:S(2)}) copy-start(f32[40,160]{1,0:T(8,128)} %param.34) | copy-start | bytes 76804
  84.3 165.4 %copy-start.10 = (f32[40,160]{1,0:T(8,128)S(1)}, f32[40,160]{1,0:T(8,128)}, u32[]{:S(2)}) copy-start(f32[40,160]{1,0:T(8,128)} %param.42) | copy-start | bytes 76804
  84.3 166.1 %copy-start.3 = (f32[640,40]{0,1:T(8,128)S(1)}, f32[640,40]{0,1:T(8,128)}, u32[]{:S(2)}) copy-start(f32[640,40]{0,1:T(8,128)} %param.33) | copy-start | bytes 307204
  84.3 166.1 %copy-start.4 = (f32[640,40]{0,1:T(8,128)S(1)}, f32[640,40]{0,1:T(8,128)}, u32[]{:S(2)}) copy-start(f32[640,40]{0,1:T(8,128)} %param.41) | copy-start | bytes 307204
  84.3 166.8 %copy-start.5 = (f32[40,640]{1,0:T(8,128)S(1)}, f32[40,640]{1,0:T(8,128)}, u32[]{:S(2)}) copy-start(f32[40,640]{1,0:T(8,128)} %param.32) | copy-start | bytes 307204
  84.4 166.8 %copy-start.6 = (f32[40,640]{1,0:T(8,128)S(1)}, f32[40,640]{1,0:T(8,128)}, u32[]{:S(2)}) copy-start(f32[40,640]{1,0:T(8,128)} %param.40) | copy-start | bytes 307204
  84.4 167.4 %copy-start.11 = (f32[40,160]{1,0:T(8,128)S(1)}, f32[40,160]{1,0:T(8,128)}, u32[]{:S(2)}) copy-start(f32[40,160]{1,0:T(8,128)} %param.36) | copy-start | bytes 76804
  84.4 167.4 %copy-start.12 = (f32[40,160]{1,0:T(8,128)S(1)}, f32[40,160]{1,0:T(8,128)}, u32[]{:S(2)}) copy-start(f32[40,160]{1,0:T(8,128)} %param.44) | copy-start | bytes 76804
  84.4 167.4 %copy-start.13 = (f32[40,160]{1,0:T(8,128)S(1)}, f32[40,160]{1,0:T(8,128)}, u32[]{:S(2)}) copy-start(f32[40,160]{1,0:T(8,128)} %param.35) | copy-start | bytes 76804
  84.4 167.4 %copy-start.14 = (f32[40,160]{1,0:T(8,128)S(1)}, f32[40,160]{1,0:T(8,128)}, u32[]{:S(2)}) copy-start(f32[40,160]{1,0:T(8,128)} %param.43) | copy-start | bytes 76804
Sparse Core Ops, SparseCore 0:
  84.6 160.2 reduce-scatter.1
